TPU v7x, 32 devices: a whole 2x2x4 slice. The times are simulated.
32 devices in a mesh: gx: 8 (over z, core), gy: 4 (over y, x).
Axes of the slice: x: 2, y: 2, z: 4, core: 2. Of those that a mesh axis runs over, the one named last changes fastest.
Arguments:
- density: float32 [128, 64, 128], P('gx', 'gy'), may hold values from 0.05 to 40, as said below
Outputs:
- potential: float32 [128, 64, 128], P('gx', 'gy')
Inputs may be any that keep to these rules, and one draw needn't show every extreme that they name: `density`: densities are positive.
All inputs are finite; a program needn't handle non-finite values.
Results may differ from a plain program's by a relative error of at most 0.00014.
Values sent between devices are 32-bit elements; how exact they have to be, the bound alone decides.
A program may use at most 64 MiB of HBM per device.

v0:
```python
import jax
import jax.numpy as jnp
from jax import lax
from jax.sharding import PartitionSpec as P

LEVELS = 4
NEWTON = 3


COUPLING = 0.1
FLOOR = 3.0


def extended(x, sides, width):
    for axis, dim in sides:
        peers, length = (lax.axis_size(axis), x.shape[dim])
        up = [(i, (i + 1) % peers) for i in range(peers)]
        down = [(j, i) for i, j in up]
        last = lax.slice_in_dim(x, length - width, length, axis=dim)
        leading = lax.slice_in_dim(x, 0, width, axis=dim)
        before = lax.ppermute(last, axis, up)
        after = lax.ppermute(leading, axis, down)
        x = jnp.concatenate([before, x, after], axis=dim)
    return x


def shifted(padded, off_x, off_y, off_z):
    size_x = padded.shape[0] - 2
    size_y = padded.shape[1] - 2
    size_z = padded.shape[2] - 2
    return padded[
        1 + off_x : 1 + off_x + size_x,
        1 + off_y : 1 + off_y + size_y,
        1 + off_z : 1 + off_z + size_z,
    ]


def hessian(padded, spacing_inv):
    center = shifted(padded, 0, 0, 0)
    pure_x = (shifted(padded, 1, 0, 0) + shifted(padded, -1, 0, 0) - 2.0 * center) * spacing_inv
    pure_y = (shifted(padded, 0, 1, 0) + shifted(padded, 0, -1, 0) - 2.0 * center) * spacing_inv
    pure_z = (shifted(padded, 0, 0, 1) + shifted(padded, 0, 0, -1) - 2.0 * center) * spacing_inv
    quarter = 0.25 * spacing_inv
    mixed_xy = (
        shifted(padded, 1, 1, 0)
        - shifted(padded, 1, -1, 0)
        - shifted(padded, -1, 1, 0)
        + shifted(padded, -1, -1, 0)
    ) * quarter
    mixed_xz = (
        shifted(padded, 1, 0, 1)
        - shifted(padded, 1, 0, -1)
        - shifted(padded, -1, 0, 1)
        + shifted(padded, -1, 0, -1)
    ) * quarter
    mixed_yz = (
        shifted(padded, 0, 1, 1)
        - shifted(padded, 0, 1, -1)
        - shifted(padded, 0, -1, 1)
        + shifted(padded, 0, -1, -1)
    ) * quarter
    return (pure_x, pure_y, pure_z, mixed_xy, mixed_xz, mixed_yz)


def nonlinear(padded, source):
    pure_x, pure_y, pure_z, mixed_xy, mixed_xz, mixed_yz = hessian(padded, 1.0)
    cubic = 2.0 * (
        pure_x * pure_y
        + pure_x * pure_z
        + pure_y * pure_z
        - mixed_xy * mixed_xy
        - mixed_xz * mixed_xz
        - mixed_yz * mixed_yz
    )
    return pure_x + pure_y + pure_z + COUPLING * cubic - source


def coefficients(padded, spacing_inv):
    pure_x, pure_y, pure_z, mixed_xy, mixed_xz, mixed_yz = hessian(padded, spacing_inv)
    stiff_x = 1.0 + 2.0 * COUPLING * (pure_y + pure_z)
    stiff_y = 1.0 + 2.0 * COUPLING * (pure_x + pure_z)
    stiff_z = 1.0 + 2.0 * COUPLING * (pure_x + pure_y)
    diagonal = jnp.maximum(2.0 * (stiff_x + stiff_y + stiff_z), FLOOR)
    relax = 1.0 / (spacing_inv * diagonal)
    return jnp.stack(
        [
            stiff_x,
            stiff_y,
            stiff_z,
            -4.0 * COUPLING * mixed_xy,
            -4.0 * COUPLING * mixed_xz,
            -4.0 * COUPLING * mixed_yz,
            relax,
        ]
    )


def jacobian(padded, weights, spacing_inv):
    parts = hessian(padded, spacing_inv)
    result = weights[0] * parts[0]
    for index in range(1, 6):
        result = result + weights[index] * parts[index]
    return result


def restrict(field):
    size_x, size_y, size_z = field.shape
    blocks = field.reshape(size_x // 2, 2, size_y // 2, 2, size_z // 2, 2)
    return jnp.sum(blocks, axis=(1, 3, 5)) * 0.125


def prolong(field):
    size_x, size_y, size_z = field.shape
    spread = jnp.broadcast_to(field[:, None, :, None, :, None], (size_x, 2, size_y, 2, size_z, 2))
    return spread.reshape(2 * size_x, 2 * size_y, 2 * size_z)


def wrap_all(field):
    return jnp.pad(field, 1, mode="wrap")


def wrap_depth(field):
    return jnp.concatenate([field[..., -1:], field, field[..., :1]], axis=-1)


def extend(field):
    return wrap_depth(extended(field, (("gx", 0), ("gy", 1)), 1))


def checker(shape, first_x, first_y, first_z):
    index_x = first_x + jnp.arange(shape[0], dtype=jnp.int32)
    index_y = first_y + jnp.arange(shape[1], dtype=jnp.int32)
    index_z = first_z + jnp.arange(shape[2], dtype=jnp.int32)
    parity = (index_x[:, None, None] + index_y[None, :, None] + index_z[None, None, :]) % 2
    return (parity == 0).astype(jnp.float32)


def black_half(change, target, weights, red_mask, pad_field, spacing_inv):
    black_mask = 1.0 - red_mask
    return (
        change
        + black_mask * (jacobian(pad_field(change), weights, spacing_inv) - target) * weights[6]
    )


def first_sweep(target, weights, red_mask, pad_field, spacing_inv):
    change = -red_mask * target * weights[6]
    return black_half(change, target, weights, red_mask, pad_field, spacing_inv)


def full_sweep(change, target, weights, red_mask, pad_field, spacing_inv):
    change = (
        change
        + red_mask * (jacobian(pad_field(change), weights, spacing_inv) - target) * weights[6]
    )
    return black_half(change, target, weights, red_mask, pad_field, spacing_inv)


def solve_coarsest(target, weights, red_mask, pad_field, spacing_inv):
    change = first_sweep(target, weights, red_mask, pad_field, spacing_inv)
    change = full_sweep(change, target, weights, red_mask, pad_field, spacing_inv)
    return change


def edge_terms():
    return None


def start_sweep(target, context):
    weights, red_mask, spacing_inv, wide = context
    return first_sweep(target, weights, red_mask, extend, spacing_inv)


def more_sweep(change, target, context):
    weights, red_mask, spacing_inv, wide = context
    return full_sweep(change, target, weights, red_mask, extend, spacing_inv)


def cycle(coarse_level, target, weight_levels, mask_levels, wide_masks):
    spacing_inv = 0.25**coarse_level
    weights = weight_levels[coarse_level]
    red_mask = mask_levels[coarse_level]
    if coarse_level == LEVELS - 1:
        packed = jnp.concatenate([weights, target[None]], axis=0)
        packed = lax.all_gather(packed, "gx", axis=1, tiled=True)
        packed = lax.all_gather(packed, "gy", axis=2, tiled=True)
        whole_mask = checker(packed.shape[1:], 0, 0, 0)
        whole = solve_coarsest(packed[7], packed[:7], whole_mask, wrap_all, spacing_inv)
        start_x = lax.axis_index("gx") * target.shape[0]
        start_y = lax.axis_index("gy") * target.shape[1]
        return lax.dynamic_slice(whole, (start_x, start_y, jnp.int32(0)), target.shape)
    context = (weights, red_mask, spacing_inv, edge_terms())
    change = start_sweep(target, context)
    leftover = target - jacobian(extend(change), weights, spacing_inv)
    change = change + prolong(
        cycle(coarse_level + 1, restrict(leftover), weight_levels, mask_levels, wide_masks)
    )
    return more_sweep(change, target, context)


def per_device(density):
    cells_total = float(density.size * lax.axis_size("gx") * lax.axis_size("gy"))
    mass_total = lax.psum(jnp.sum(density), ("gx", "gy"))
    source = density / (mass_total / cells_total) - 1.0
    mask_levels = []
    wide_masks = []
    for coarse_level in range(LEVELS):
        shape = (
            density.shape[0] >> coarse_level,
            density.shape[1] >> coarse_level,
            density.shape[2] >> coarse_level,
        )
        start_x = lax.axis_index("gx") * shape[0]
        start_y = lax.axis_index("gy") * shape[1]
        mask_levels.append(checker(shape, start_x, start_y, 0))
        wide_shape = (shape[0] + 2, shape[1] + 2, shape[2] + 2)
        wide_masks.append(checker(wide_shape, start_x - 1, start_y - 1, -1))

    def newton_turn(newton_step, potential):
        padded_levels = []
        coarse = potential
        for coarse_level in range(LEVELS):
            if coarse_level > 0:
                coarse = restrict(coarse)
            padded_levels.append(extend(coarse))
        weight_levels = [
            coefficients(padded_levels[coarse_level], 0.25**coarse_level)
            for coarse_level in range(LEVELS)
        ]
        target = -nonlinear(padded_levels[0], source)
        return potential + cycle(0, target, weight_levels, mask_levels, wide_masks)

    return lax.fori_loop(0, NEWTON, newton_turn, jnp.zeros_like(density))


def solution(mesh):
    placed = (P("gx", "gy", None),)
    return jax.shard_map(
        per_device, mesh=mesh, in_specs=placed, out_specs=P("gx", "gy", None), check_vma=False
    )
```

profile of v0, /device:TPU:0, one launch (start us, length us, event | category | flops | bytes accessed | tf_op | source)
XLA Modules:
  0.0 727.7 jit_solution(4826400900629721583)
XLA Ops:
  1.6 42.1 %psum.7 = f32[]{:T(128)} all-reduce(f32[]{:T(128)} %reduce_sum.87), channel_id=1, replica_groups=mesh['gx'=8,'gy'=4] {'gx','gy'}, use_global_device_ids=true, to_apply=%region_1.0 | all-reduce | flops 1 | bytes 8 | tf_op jit(solution)/shard_map/psum | solution.py:203
  45.5 681.6 %while.16 = (s32[]{:T(128)}, f32[16,16,128]{2,1,0:T(8,128)S(1)}, f32[16,16,128]{2,1,0:T(8,128)S(1)}, s32[16,16]{1,0:T(8,128)S(1)}, s32[8,8]{1,0:T(8,128)S(1)}, /...) while((s32[]{:T(128)}, f32[16,16,128]{2,1,0:T(8,128)S(1)}, ...), condition=%wide.region_9.10_spmd.clone.clone.clone, body=%wide.region_2.9_spmd.clone.clone.clone.sunk | while | flops 16571231 | bytes 33015364 | solution.py:233
  46.6 9.8 %reshape.245 = f32[8,2,8,2,64,2]{5,4,3,2,1,0:T(8,128)} reshape(f32[16,16,128]{2,1,0:T(8,128)S(1)} %broadcast_select_fusion.2) | data formatting | bytes 262144 | tf_op jit(solution)/shard_map/while/body/eval_jaxpr/reshape | solution.py:108
  56.3 4.0 reduce_sum.113
  60.4 3.6 collective-permute-start.12
  77.6 4.4 collective-permute-done.25
  104.5 3.6 collective-permute-done.9
  113.6 9.8 %reshape.244 = f32[8,2,8,2,64,2]{5,4,3,2,1,0:T(8,128)} reshape(f32[16,16,128]{2,1,0:T(8,128)S(1)} %fusion.533) | data formatting | bytes 262144 | tf_op jit(solution)/shard_map/while/body/eval_jaxpr/reshape | solution.py:108
  123.4 4.0 reduce_sum.112
  171.9 12.8 %all_gather.22 = f32[8,16,2,16]{3,2,1,0:T(2,128)S(1)} all-gather(f32[8,2,2,16]{3,2,1,0:T(2,128)S(1)} %constant_dynamic-update-slice_fusion.23), channel_id=1, replica_groups=mesh['gx'=8,'gy'=4] {'gx'}, dimensions={1}, use_global_device_ids=true | all-gather | bytes 18432 | tf_op jit(solution)/shard_map/while/body/eval_jaxpr/all_gather | solution.py:185
  184.7 9.9 %all_gather.23 = f32[8,16,8,16]{3,1,0,2:T(8,128)S(1)} all-gather(f32[8,16,2,16]{3,1,0,2:T(8,128)S(1)} %copy.20), channel_id=1, replica_groups=mesh['gx'=8,'gy'=4] {'gy'}, dimensions={2}, use_global_device_ids=true | all-gather | bytes 81920 | tf_op jit(solution)/shard_map/while/body/eval_jaxpr/all_gather | solution.py:186
  240.3 4.0 broadcast_in_dim.61
  244.3 6.9 reshape.250
  252.7 3.6 collective-permute-done.57
  274.4 9.8 %reshape.245 = f32[8,2,8,2,64,2]{5,4,3,2,1,0:T(8,128)} reshape(f32[16,16,128]{2,1,0:T(8,128)S(1)} %broadcast_select_fusion.2) | data formatting | bytes 262144 | tf_op jit(solution)/shard_map/while/body/eval_jaxpr/reshape | solution.py:108
  284.2 4.0 reduce_sum.113
  304.2 4.4 collective-permute-done.25
  340.2 9.8 %reshape.244 = f32[8,2,8,2,64,2]{5,4,3,2,1,0:T(8,128)} reshape(f32[16,16,128]{2,1,0:T(8,128)S(1)} %fusion.533) | data formatting | bytes 262144 | tf_op jit(solution)/shard_map/while/body/eval_jaxpr/reshape | solution.py:108
  350.0 4.0 reduce_sum.112
  398.5 12.8 %all_gather.22 = f32[8,16,2,16]{3,2,1,0:T(2,128)S(1)} all-gather(f32[8,2,2,16]{3,2,1,0:T(2,128)S(1)} %constant_dynamic-update-slice_fusion.23), channel_id=1, replica_groups=mesh['gx'=8,'gy'=4] {'gx'}, dimensions={1}, use_global_device_ids=true | all-gather | bytes 18432 | tf_op jit(solution)/shard_map/while/body/eval_jaxpr/all_gather | solution.py:185
  411.4 9.9 %all_gather.23 = f32[8,16,8,16]{3,1,0,2:T(8,128)S(1)} all-gather(f32[8,16,2,16]{3,1,0,2:T(8,128)S(1)} %copy.20), channel_id=1, replica_groups=mesh['gx'=8,'gy'=4] {'gy'}, dimensions={2}, use_global_device_ids=true | all-gather | bytes 81920 | tf_op jit(solution)/shard_map/while/body/eval_jaxpr/all_gather | solution.py:186
  467.0 4.0 broadcast_in_dim.61
  471.0 6.9 reshape.250
  501.0 9.8 %reshape.245 = f32[8,2,8,2,64,2]{5,4,3,2,1,0:T(8,128)} reshape(f32[16,16,128]{2,1,0:T(8,128)S(1)} %broadcast_select_fusion.2) | data formatting | bytes 262144 | tf_op jit(solution)/shard_map/while/body/eval_jaxpr/reshape | solution.py:108
  510.8 4.0 reduce_sum.113
  530.8 4.4 collective-permute-done.25
  566.9 9.8 %reshape.244 = f32[8,2,8,2,64,2]{5,4,3,2,1,0:T(8,128)} reshape(f32[16,16,128]{2,1,0:T(8,128)S(1)} %fusion.533) | data formatting | bytes 262144 | tf_op jit(solution)/shard_map/while/body/eval_jaxpr/reshape | solution.py:108
  576.7 4.0 reduce_sum.112
  625.1 12.8 %all_gather.22 = f32[8,16,2,16]{3,2,1,0:T(2,128)S(1)} all-gather(f32[8,2,2,16]{3,2,1,0:T(2,128)S(1)} %constant_dynamic-update-slice_fusion.23), channel_id=1, replica_groups=mesh['gx'=8,'gy'=4] {'gx'}, dimensions={1}, use_global_device_ids=true | all-gather | bytes 18432 | tf_op jit(solution)/shard_map/while/body/eval_jaxpr/all_gather | solution.py:185
  638.0 9.9 %all_gather.23 = f32[8,16,8,16]{3,1,0,2:T(8,128)S(1)} all-gather(f32[8,16,2,16]{3,1,0,2:T(8,128)S(1)} %copy.20), channel_id=1, replica_groups=mesh['gx'=8,'gy'=4] {'gy'}, dimensions={2}, use_global_device_ids=true | all-gather | bytes 81920 | tf_op jit(solution)/shard_map/while/body/eval_jaxpr/all_gather | solution.py:186
  693.6 4.0 broadcast_in_dim.61
  697.6 6.9 reshape.250
  (890 shorter events, 474.3 us)
Async XLA Ops:
  45.5 36.6 %collective-permute-start = (f32[1,16,128]{2,1,0:T(8,128)S(1)}, f32[1,16,128]{2,1,0:T(8,128)S(1)}, u32[]{:S(2)}, u32[]{:S(2)}) collective-permute-start(f32[1,16,128]{2,1,0:T(8,128)S(1)} %get-tuple-element.745), channel_id=1, source_target_pairs={{4,0},{8,4},{12,8},{16,12},{20,16},{24,20},{28,24},{0,28},{5,1},{9... | collective-permute-start | bytes 24584 | tf_op jit(solution)/shard_map/while/body/eval_jaxpr/ppermute | solution.py:22
  46.6 37.6 %collective-permute-start.1 = (f32[1,16,128]{2,1,0:T(8,128)S(1)}, f32[1,16,128]{2,1,0:T(8,128)S(1)}, u32[]{:S(2)}, u32[]{:S(2)}) collective-permute-start(f32[1,16,128]{2,1,0:T(8,128)S(1)} %get-tuple-element.746), channel_id=1, source_target_pairs={{0,4},{4,8},{8,12},{12,16},{16,20},{20,24},{24,28},{28,0},{1,5},{5... | collective-permute-start | bytes 24584 | tf_op jit(solution)/shard_map/while/body/eval_jaxpr/ppermute | solution.py:21
  60.4 24.8 %collective-permute-start.12 = (f32[1,8,64]{2,1,0:T(8,128)S(1)}, f32[1,8,64]{2,1,0:T(8,128)S(1)}, u32[]{:S(2)}, u32[]{:S(2)}) collective-permute-start(f32[1,8,64]{2,1,0:T(8,128)S(1)} %get-tuple-element.785), channel_id=1, source_target_pairs={{4,0},{8,4},{12,8},{16,12},{20,16},{24,20},{28,24},{0,28},{5,1},{9... | collective-permute-start | bytes 6152 | tf_op jit(solution)/shard_map/while/body/eval_jaxpr/ppermute | solution.py:22
  77.5 8.7 %collective-permute-start.13 = (f32[1,8,64]{2,1,0:T(8,128)S(1)}, f32[1,8,64]{2,1,0:T(8,128)S(1)}, u32[]{:S(2)}, u32[]{:S(2)}) collective-permute-start(f32[1,8,64]{2,1,0:T(8,128)S(1)} %get-tuple-element.786), channel_id=1, source_target_pairs={{0,4},{4,8},{8,12},{12,16},{16,20},{20,24},{24,28},{28,0},{1,5},{5... | collective-permute-start | bytes 6152 | tf_op jit(solution)/shard_map/while/body/eval_jaxpr/ppermute | solution.py:21
  82.0 46.0 %collective-permute-start.26 = (f32[6,1,32]{2,1,0:T(1,128)S(1)}, f32[6,1,32]{2,1,0:T(1,128)S(1)}, u32[]{:S(2)}, u32[]{:S(2)}) collective-permute-start(f32[6,1,32]{2,1,0:T(1,128)S(1)} %get-tuple-element.825), channel_id=1, source_target_pairs={{1,0},{2,1},{3,2},{0,3},{5,4},{6,5},{7,6},{4,7},{9,8},{10,9},{11,1... | collective-permute-start | bytes 2312 | tf_op jit(solution)/shard_map/while/body/eval_jaxpr/ppermute | solution.py:22
  82.1 46.0 %collective-permute-start.27 = (f32[6,1,32]{2,1,0:T(1,128)S(1)}, f32[6,1,32]{2,1,0:T(1,128)S(1)}, u32[]{:S(2)}, u32[]{:S(2)}) collective-permute-start(f32[6,1,32]{2,1,0:T(1,128)S(1)} %get-tuple-element.826), channel_id=1, source_target_pairs={{0,1},{1,2},{2,3},{3,0},{4,5},{5,6},{6,7},{7,4},{8,9},{9,10},{10,1... | collective-permute-start | bytes 2312 | tf_op jit(solution)/shard_map/while/body/eval_jaxpr/ppermute | solution.py:21
  90.8 4.9 collective-permute-start.5
  103.2 4.9 collective-permute-start.9
  138.6 4.9 collective-permute-start.21
  218.8 4.9 collective-permute-start.49
  251.3 4.9 collective-permute-start.57
  263.3 4.9 collective-permute-start.61
  273.8 35.0 %collective-permute-start = (f32[1,16,128]{2,1,0:T(8,128)S(1)}, f32[1,16,128]{2,1,0:T(8,128)S(1)}, u32[]{:S(2)}, u32[]{:S(2)}) collective-permute-start(f32[1,16,128]{2,1,0:T(8,128)S(1)} %get-tuple-element.745), channel_id=1, source_target_pairs={{4,0},{8,4},{12,8},{16,12},{20,16},{24,20},{28,24},{0,28},{5,1},{9... | collective-permute-start | bytes 24584 | tf_op jit(solution)/shard_map/while/body/eval_jaxpr/ppermute | solution.py:22
  273.9 36.8 %collective-permute-start.1 = (f32[1,16,128]{2,1,0:T(8,128)S(1)}, f32[1,16,128]{2,1,0:T(8,128)S(1)}, u32[]{:S(2)}, u32[]{:S(2)}) collective-permute-start(f32[1,16,128]{2,1,0:T(8,128)S(1)} %get-tuple-element.746), channel_id=1, source_target_pairs={{0,4},{4,8},{8,12},{12,16},{16,20},{20,24},{24,28},{28,0},{1,5},{5... | collective-permute-start | bytes 24584 | tf_op jit(solution)/shard_map/while/body/eval_jaxpr/ppermute | solution.py:21
  288.2 23.6 %collective-permute-start.12 = (f32[1,8,64]{2,1,0:T(8,128)S(1)}, f32[1,8,64]{2,1,0:T(8,128)S(1)}, u32[]{:S(2)}, u32[]{:S(2)}) collective-permute-start(f32[1,8,64]{2,1,0:T(8,128)S(1)} %get-tuple-element.785), channel_id=1, source_target_pairs={{4,0},{8,4},{12,8},{16,12},{20,16},{24,20},{28,24},{0,28},{5,1},{9... | collective-permute-start | bytes 6152 | tf_op jit(solution)/shard_map/while/body/eval_jaxpr/ppermute | solution.py:22
  304.1 8.7 %collective-permute-start.13 = (f32[1,8,64]{2,1,0:T(8,128)S(1)}, f32[1,8,64]{2,1,0:T(8,128)S(1)}, u32[]{:S(2)}, u32[]{:S(2)}) collective-permute-start(f32[1,8,64]{2,1,0:T(8,128)S(1)} %get-tuple-element.786), channel_id=1, source_target_pairs={{0,4},{4,8},{8,12},{12,16},{16,20},{20,24},{24,28},{28,0},{1,5},{5... | collective-permute-start | bytes 6152 | tf_op jit(solution)/shard_map/while/body/eval_jaxpr/ppermute | solution.py:21
  308.6 46.1 %collective-permute-start.26 = (f32[6,1,32]{2,1,0:T(1,128)S(1)}, f32[6,1,32]{2,1,0:T(1,128)S(1)}, u32[]{:S(2)}, u32[]{:S(2)}) collective-permute-start(f32[6,1,32]{2,1,0:T(1,128)S(1)} %get-tuple-element.825), channel_id=1, source_target_pairs={{1,0},{2,1},{3,2},{0,3},{5,4},{6,5},{7,6},{4,7},{9,8},{10,9},{11,1... | collective-permute-start | bytes 2312 | tf_op jit(solution)/shard_map/while/body/eval_jaxpr/ppermute | solution.py:22
  308.8 45.9 %collective-permute-start.27 = (f32[6,1,32]{2,1,0:T(1,128)S(1)}, f32[6,1,32]{2,1,0:T(1,128)S(1)}, u32[]{:S(2)}, u32[]{:S(2)}) collective-permute-start(f32[6,1,32]{2,1,0:T(1,128)S(1)} %get-tuple-element.826), channel_id=1, source_target_pairs={{0,1},{1,2},{2,3},{3,0},{4,5},{5,6},{6,7},{7,4},{8,9},{9,10},{10,1... | collective-permute-start | bytes 2312 | tf_op jit(solution)/shard_map/while/body/eval_jaxpr/ppermute | solution.py:21
  317.4 4.9 collective-permute-start.5
  329.8 4.9 collective-permute-start.9
  478.0 4.9 collective-permute-start.57
  489.9 4.9 collective-permute-start.61
  500.5 35.0 %collective-permute-start = (f32[1,16,128]{2,1,0:T(8,128)S(1)}, f32[1,16,128]{2,1,0:T(8,128)S(1)}, u32[]{:S(2)}, u32[]{:S(2)}) collective-permute-start(f32[1,16,128]{2,1,0:T(8,128)S(1)} %get-tuple-element.745), channel_id=1, source_target_pairs={{4,0},{8,4},{12,8},{16,12},{20,16},{24,20},{28,24},{0,28},{5,1},{9... | collective-permute-start | bytes 24584 | tf_op jit(solution)/shard_map/while/body/eval_jaxpr/ppermute | solution.py:22
  500.5 36.8 %collective-permute-start.1 = (f32[1,16,128]{2,1,0:T(8,128)S(1)}, f32[1,16,128]{2,1,0:T(8,128)S(1)}, u32[]{:S(2)}, u32[]{:S(2)}) collective-permute-start(f32[1,16,128]{2,1,0:T(8,128)S(1)} %get-tuple-element.746), channel_id=1, source_target_pairs={{0,4},{4,8},{8,12},{12,16},{16,20},{20,24},{24,28},{28,0},{1,5},{5... | collective-permute-start | bytes 24584 | tf_op jit(solution)/shard_map/while/body/eval_jaxpr/ppermute | solution.py:21
  514.9 23.6 %collective-permute-start.12 = (f32[1,8,64]{2,1,0:T(8,128)S(1)}, f32[1,8,64]{2,1,0:T(8,128)S(1)}, u32[]{:S(2)}, u32[]{:S(2)}) collective-permute-start(f32[1,8,64]{2,1,0:T(8,128)S(1)} %get-tuple-element.785), channel_id=1, source_target_pairs={{4,0},{8,4},{12,8},{16,12},{20,16},{24,20},{28,24},{0,28},{5,1},{9... | collective-permute-start | bytes 6152 | tf_op jit(solution)/shard_map/while/body/eval_jaxpr/ppermute | solution.py:22
  530.7 8.7 %collective-permute-start.13 = (f32[1,8,64]{2,1,0:T(8,128)S(1)}, f32[1,8,64]{2,1,0:T(8,128)S(1)}, u32[]{:S(2)}, u32[]{:S(2)}) collective-permute-start(f32[1,8,64]{2,1,0:T(8,128)S(1)} %get-tuple-element.786), channel_id=1, source_target_pairs={{0,4},{4,8},{8,12},{12,16},{16,20},{20,24},{24,28},{28,0},{1,5},{5... | collective-permute-start | bytes 6152 | tf_op jit(solution)/shard_map/while/body/eval_jaxpr/ppermute | solution.py:21
  535.3 46.1 %collective-permute-start.26 = (f32[6,1,32]{2,1,0:T(1,128)S(1)}, f32[6,1,32]{2,1,0:T(1,128)S(1)}, u32[]{:S(2)}, u32[]{:S(2)}) collective-permute-start(f32[6,1,32]{2,1,0:T(1,128)S(1)} %get-tuple-element.825), channel_id=1, source_target_pairs={{1,0},{2,1},{3,2},{0,3},{5,4},{6,5},{7,6},{4,7},{9,8},{10,9},{11,1... | collective-permute-start | bytes 2312 | tf_op jit(solution)/shard_map/while/body/eval_jaxpr/ppermute | solution.py:22
  535.5 45.9 %collective-permute-start.27 = (f32[6,1,32]{2,1,0:T(1,128)S(1)}, f32[6,1,32]{2,1,0:T(1,128)S(1)}, u32[]{:S(2)}, u32[]{:S(2)}) collective-permute-start(f32[6,1,32]{2,1,0:T(1,128)S(1)} %get-tuple-element.826), channel_id=1, source_target_pairs={{0,1},{1,2},{2,3},{3,0},{4,5},{5,6},{6,7},{7,4},{8,9},{9,10},{10,1... | collective-permute-start | bytes 2312 | tf_op jit(solution)/shard_map/while/body/eval_jaxpr/ppermute | solution.py:21
  544.1 4.9 collective-permute-start.5
  556.5 4.9 collective-permute-start.9
  704.6 4.9 collective-permute-start.57
  716.6 4.9 collective-permute-start.61
  (161 other events, 574.7 us)
where the time goes:
time: 728 us
  waiting for transfers between devices  316 us (43%)
  starting transfers between devices  136 us (19%)
  blocking collectives  110 us (15%)
  local copies, waits for them, and re-layouts  107 us (15%)
  other arithmetic  54.1 us (7%)
    ppermute x96, waiting for transfers between devices, extended(): before = lax.ppermute(last, axis, up)  226 us
    ppermute x96, waiting for transfers between devices, extended(): after = lax.ppermute(leading, axis, down)  89.7 us
    ppermute x96, starting transfers between devices, extended(): before = lax.ppermute(last, axis, up)  77 us
    reshape x12, local copies, waits for them, and re-layouts, restrict(): blocks = field.reshape(size_x // 2, 2, size_y // 2, 2, size_z // 2, 2)  62.2 us
    ppermute x96, starting transfers between devices, extended(): after = lax.ppermute(leading, axis, down)  59.4 us
    psum x1, blocking collectives, per_device(): mass_total = lax.psum(jnp.sum(density), ('gx', 'gy'))  42.1 us
    all_gather x3, blocking collectives, cycle(): packed = lax.all_gather(packed, 'gx', axis=1, tiled=True)  38.5 us
    all_gather x3, blocking collectives, cycle(): packed = lax.all_gather(packed, 'gy', axis=2, tiled=True)  29.6 us
  transfers between devices with their start and end apart: 192, of which 162 were waited for; matrix products, arithmetic and copies ran while one was open for 14% of the time, Pallas kernels for 0%

commit v1 on v0

v1 whole, which is shorter than its diff:
```python
import functools

import jax
import jax.numpy as jnp
from jax import lax
from jax.experimental import pallas as pl
from jax.experimental.pallas import tpu as pltpu
from jax.sharding import PartitionSpec as P

LEVELS = 4
NEWTON = 3
COUPLING = 0.1
FLOOR = 3.0
HALO = 8
MESH = pl.DeviceIdType.MESH


def parts_of(block, step):
    rows, lanes = block.shape[1], block.shape[2]
    center = block[1:-1]
    twice = center + center
    z_next = pltpu.roll(block, lanes - step, 2)
    z_prev = pltpu.roll(block, step, 2)
    y_next = pltpu.roll(block, rows - 1, 1)
    y_prev = pltpu.roll(block, 1, 1)
    slope_z = z_next - z_prev
    slope_y = y_next - y_prev
    xx = block[2:] + block[:-2] - twice
    yy = y_next[1:-1] + y_prev[1:-1] - twice
    zz = z_next[1:-1] + z_prev[1:-1] - twice
    xy = slope_y[2:] - slope_y[:-2]
    xz = slope_z[2:] - slope_z[:-2]
    inner = slope_z[1:-1]
    yz = pltpu.roll(inner, rows - 1, 1) - pltpu.roll(inner, 1, 1)
    return center, xx, yy, zz, xy, xz, yz


def red_of(shape, first, level):
    total = (
        lax.broadcasted_iota(jnp.int32, shape, 0)
        + first
        + lax.broadcasted_iota(jnp.int32, shape, 1)
        + (lax.broadcasted_iota(jnp.int32, shape, 2) >> level)
    )
    return (total & 1) == 0


def planes(first, count, body):
    size = 4 if count % 4 == 0 else 2
    assert count % size == 0

    def turn(i, carry):
        body(first + i * size, size)
        return carry

    lax.fori_loop(0, count // size, turn, 0)


class Level:
    def __init__(self, level, pad, weights, target, va, vb):
        self.level, self.pad = level, pad
        self.weights, self.target, self.va, self.vb = weights, target, va, vb
        self.step = 1 << level
        self.scale = 0.25**level

    def setup(self, u_ref, first, count, source_ref=None):
        def body(at, size):
            block = u_ref[pl.ds(at - 1, size + 2)]
            _, xx, yy, zz, xy, xz, yz = parts_of(block, self.step)
            if self.level > 0:
                xx, yy, zz = xx * self.scale, yy * self.scale, zz * self.scale
            quarter = 0.25 * self.scale
            xy, xz, yz = xy * quarter, xz * quarter, yz * quarter
            kx = 1.0 + 2.0 * COUPLING * (yy + zz)
            ky = 1.0 + 2.0 * COUPLING * (xx + zz)
            kz = 1.0 + 2.0 * COUPLING * (xx + yy)
            diagonal = jnp.maximum(2.0 * (kx + ky + kz), FLOOR)
            relax = 1.0 / (self.scale * diagonal)
            rows = pl.ds(at, size)
            if source_ref is not None:
                cubic = 2.0 * (xx * yy + xx * zz + yy * zz - xy * xy - xz * xz - yz * yz)
                target = source_ref[rows] - (xx + yy + zz + COUPLING * cubic)
                self.target[rows] = target
            else:
                target = self.target[rows]
            mixed = -4.0 * COUPLING * quarter
            self.weights[0, rows] = kx * self.scale
            self.weights[1, rows] = ky * self.scale
            self.weights[2, rows] = kz * self.scale
            self.weights[3, rows] = xy * mixed
            self.weights[4, rows] = xz * mixed
            self.weights[5, rows] = yz * mixed
            self.weights[6, rows] = relax
            red = red_of(target.shape, (first - self.pad) % 2, self.level)
            self.va[rows] = jnp.where(red, -target * relax, 0.0)

        planes(first, count, body)

    def excess(self, v_ref, at, size):
        block = v_ref[pl.ds(at - 1, size + 2)]
        center, xx, yy, zz, xy, xz, yz = parts_of(block, self.step)
        rows = pl.ds(at, size)
        w = self.weights
        total = w[0, rows] * xx + w[1, rows] * yy + w[2, rows] * zz
        total += w[3, rows] * xy + w[4, rows] * xz + w[5, rows] * yz
        return total - self.target[rows], center

    def half(self, src, first, count, red, put):
        def body(at, size):
            excess, center = self.excess(src, at, size)
            change = excess * self.weights[6, pl.ds(at, size)]
            mask = red_of(change.shape, (first - self.pad) % 2, self.level)
            if red:
                value = jnp.where(mask, center + change, center)
            else:
                value = jnp.where(mask, center, center + change)
            put(at, size, value)

        planes(first, count, body)


def store_to(ref):
    def put(at, size, value):
        ref[pl.ds(at, size)] = value

    return put


def pair_xz(value, step):
    size, rows, lanes = value.shape
    halves = value.reshape(size // 2, 2, rows, lanes)
    value = halves[:, 0] + halves[:, 1]
    lane = lax.broadcasted_iota(jnp.int32, value.shape, 2)
    other = jnp.where(
        (lane & step) == 0, pltpu.roll(value, lanes - step, 2), pltpu.roll(value, step, 2)
    )
    return value + other


def pair_y(tmp, first, count, rows, out, out_first, out_row):
    half = rows // 2

    def body(i, carry):
        low = tmp[first + i, pl.ds(0, half, stride=2), :]
        high = tmp[first + i, pl.ds(1, half, stride=2), :]
        out[out_first + i, pl.ds(out_row, half), :] = (low + high) * 0.125
        return carry

    lax.fori_loop(0, count, body, 0)


def wrap_planes(ref, pad, count):
    for i in range(pad):
        ref[i] = ref[count + i]
        ref[pad + count + i] = ref[pad + i]


def kernel(
    gx, gy, density_ref, out_ref,
    S, U, W0, T0, A0, B0, R0,
    U1, W1, T1, A1, B1, X1, R1,
    U2, W2, T2, A2, B2, R2,
    U3, W3, T3, A3, B3,
    G,
    near_send, near_recv, mid_send, mid_recv, row_send, row_recv, col_send, col_recv,
):
    bx, by, nz = density_ref.shape
    me_x, me_y = lax.axis_index("gx"), lax.axis_index("gy")
    pad1 = HALO // 2
    b1x, b1y = bx // 2, by // 2
    b2x, b2y = bx // 4, by // 4
    n2x, n2y = b2x * gx, b2y * gy
    n3x, n3y = n2x // 2, n2y // 2
    row1 = HALO

    def device(dx, dy):
        return (lax.rem(me_x + dx + gx, gx), lax.rem(me_y + dy + gy, gy))

    around = [(dx, dy) for dx in (-1, 0, 1) for dy in (-1, 0, 1) if (dx, dy) != (0, 0)]
    friends = [device(d, 0) for d in range(1, gx)]
    friends += [device(0, d) for d in range(1, gy)]
    friends += [device(dx, dy) for dx, dy in around if dx and dy]
    barrier = pltpu.get_barrier_semaphore()
    for friend in friends:
        pl.semaphore_signal(barrier, inc=1, device_id=friend, device_id_type=MESH)
    pl.semaphore_wait(barrier, len(friends))

    def spans(d, block, halo):
        if d == 0:
            return (halo, halo, block)
        if d == 1:
            return (block, 0, halo)
        return (halo, block + halo, halo)

    def exchange(ref, block_x, halo_x, block_y, halo_y, send, recv, turn):
        copies = []
        for index, (dx, dy) in enumerate(around):
            sx, rx, cx = spans(dx, block_x, halo_x)
            sy, ry, cy = spans(dy, block_y, halo_y)
            copy = pltpu.make_async_remote_copy(
                src_ref=ref.at[pl.ds(sx, cx), pl.ds(sy, cy)],
                dst_ref=ref.at[pl.ds(rx, cx), pl.ds(ry, cy)],
                send_sem=send.at[turn, index],
                recv_sem=recv.at[turn, index],
                device_id=device(dx, dy),
                device_id_type=MESH,
            )
            copy.start()
            copies.append(copy)
        return copies

    def gather(slot):
        copies = []
        for d in range(1, gx):
            copy = pltpu.make_async_remote_copy(
                src_ref=G.at[slot, me_y, me_x],
                dst_ref=G.at[slot, me_y, me_x],
                send_sem=row_send.at[slot, d - 1],
                recv_sem=row_recv.at[slot, d - 1],
                device_id=device(d, 0),
                device_id_type=MESH,
            )
            copy.start()
            copies.append(copy)
        for copy in copies:
            copy.wait()
        copies = []
        for d in range(1, gy):
            copy = pltpu.make_async_remote_copy(
                src_ref=G.at[slot, me_y],
                dst_ref=G.at[slot, me_y],
                send_sem=col_send.at[slot, d - 1],
                recv_sem=col_recv.at[slot, d - 1],
                device_id=device(0, d),
                device_id_type=MESH,
            )
            copy.start()
            copies.append(copy)
        for copy in copies:
            copy.wait()

    own = density_ref[...]
    S[pl.ds(HALO, bx), pl.ds(HALO, by)] = own
    halo_copies = exchange(S, bx, HALO, by, HALO, near_send, near_recv, NEWTON - 1)
    part = jnp.sum(own, axis=0)
    tiles = part[0:8]
    for t in range(1, by // 8):
        tiles = tiles + part[8 * t : 8 * t + 8]
    G[NEWTON, me_y, me_x] = tiles
    U[...] = jnp.zeros_like(U)
    gather(NEWTON)
    mass = jnp.sum(G[NEWTON], axis=(0, 1))
    mass = jnp.sum(jnp.sum(mass, axis=0, keepdims=True), axis=1, keepdims=True)
    mean = mass / float(bx * gx * by * gy * nz)
    for copy in halo_copies:
        copy.wait()

    def to_source(i, carry):
        S[i] = S[i] / mean - 1.0
        return carry

    lax.fori_loop(0, bx + 2 * HALO, to_source, 0)

    L0 = Level(0, HALO, W0, T0, A0, B0)
    L1 = Level(1, pad1, W1, T1, A1, B1)
    L2 = Level(2, 2, W2, T2, A2, B2)
    L3 = Level(3, 2, W3, T3, A3, B3)

    lane_in = lax.broadcasted_iota(jnp.int32, (nz, nz), 0)
    lane_out = lax.broadcasted_iota(jnp.int32, (nz, nz), 1)
    width = nz // 4

    def dot(a, b):
        return lax.dot_general(
            a, b, (((1,), (0,)), ((), ())),
            precision=lax.Precision.HIGHEST, preferred_element_type=jnp.float32,
        )

    def newton(k, carry):
        L0.setup(U, 2, bx + 12, S)
        L0.half(A0, 3, bx + 10, False, store_to(B0))

        def leftover0(at, size):
            excess, _ = L0.excess(B0, at, size)
            R0[pl.ds(at // 2, size // 2)] = pair_xz(-excess, 1)

        planes(4, bx + 8, leftover0)
        pair_y(R0, 2, b1x + 4, by + 2 * HALO, T1, 2, row1 - pad1)

        def shrink0(at, size):
            R0[pl.ds(at // 2, size // 2)] = pair_xz(U[pl.ds(at, size)], 1)

        planes(0, bx + 2 * HALO, shrink0)
        pair_y(R0, 0, b1x + 2 * pad1, by + 2 * HALO, U1, 0, row1 - pad1)

        L1.setup(U1, 2, b1x + 4)
        L1.half(A1, 3, b1x + 2, False, store_to(B1))
        X1[pl.ds(pad1, b1x), pl.ds(row1, b1y)] = B1[pl.ds(pad1, b1x), pl.ds(row1, b1y)]
        mid_copies = exchange(X1, b1x, pad1, b1y, row1, mid_send, mid_recv, k)

        def leftover1(at, size):
            excess, _ = L1.excess(B1, at, size)
            R1[pl.ds((at - pad1) // 2, size // 2)] = pair_xz(-excess, 2)

        planes(pad1, b1x, leftover1)

        def shrink1(at, size):
            R1[pl.ds(b2x + (at - pad1) // 2, size // 2)] = pair_xz(U1[pl.ds(at, size)], 2)

        planes(pad1, b1x, shrink1)

        message = None
        for i in range(b2x):
            rows = []
            for which in range(2):
                low = R1[which * b2x + i, pl.ds(row1, b2y, stride=2), :]
                high = R1[which * b2x + i, pl.ds(row1 + 1, b2y, stride=2), :]
                rows.append((low + high) * 0.125)
            pick = ((lane_in & 3) == 0) & ((lane_in >> 2) + i * width == lane_out)
            term = dot(jnp.concatenate(rows, axis=0), pick.astype(jnp.float32))
            message = term if message is None else message + term
        G[k, me_y, me_x] = message
        gather(k)

        packed = G[k].reshape(gy * gx * 2 * b2y, nz)
        rights, fields = [], []
        for i in range(b2x):
            spread = (lane_in == (lane_out >> 2) + i * width).astype(jnp.float32)
            cells = dot(packed, spread).reshape(gy, gx, 2 * b2y, nz)
            rights.append(jnp.concatenate([cells[j, :, :b2y] for j in range(gy)], axis=1))
            fields.append(jnp.concatenate([cells[j, :, b2y:] for j in range(gy)], axis=1))
        T2[pl.ds(2, n2x)] = jnp.stack(rights, axis=1).reshape(n2x, n2y, nz)
        U2[pl.ds(2, n2x)] = jnp.stack(fields, axis=1).reshape(n2x, n2y, nz)
        wrap_planes(U2, 2, n2x)

        L2.setup(U2, 2, n2x)
        wrap_planes(A2, 2, n2x)
        L2.half(A2, 2, n2x, False, store_to(B2))
        wrap_planes(B2, 2, n2x)

        def leftover2(at, size):
            excess, _ = L2.excess(B2, at, size)
            R2[pl.ds((at - 2) // 2, size // 2)] = pair_xz(-excess, 4)

        planes(2, n2x, leftover2)
        pair_y(R2, 0, n3x, n2y, T3, 2, 0)

        def shrink2(at, size):
            R2[pl.ds((at - 2) // 2, size // 2)] = pair_xz(U2[pl.ds(at, size)], 4)

        planes(2, n2x, shrink2)
        pair_y(R2, 0, n3x, n2y, U3, 2, 0)
        wrap_planes(U3, 2, n3x)
        L3.setup(U3, 2, n3x)
        wrap_planes(A3, 2, n3x)
        L3.half(A3, 2, n3x, False, store_to(B3))
        wrap_planes(B3, 2, n3x)
        L3.half(B3, 2, n3x, True, store_to(A3))
        wrap_planes(A3, 2, n3x)
        L3.half(A3, 2, n3x, False, store_to(B3))

        def rise3(i, carry):
            value = B3[2 + i]
            R2[i, pl.ds(0, n3y, stride=2), :] = value
            R2[i, pl.ds(1, n3y, stride=2), :] = value
            both = R2[i]
            B2[2 + 2 * i] = B2[2 + 2 * i] + both
            B2[3 + 2 * i] = B2[3 + 2 * i] + both
            return carry

        lax.fori_loop(0, n3x, rise3, 0)
        wrap_planes(B2, 2, n2x)
        L2.half(B2, 2, n2x, True, store_to(A2))
        wrap_planes(A2, 2, n2x)
        L2.half(A2, 2, n2x, False, store_to(B2))
        wrap_planes(B2, 2, n2x)

        for copy in mid_copies:
            copy.wait()
        near = b2y + 4
        shift = lax.rem(n2y - me_y * b2y + 2, n2y)

        def rise2(i, carry):
            value = pltpu.roll(B2[me_x * b2x + i], shift, 0)[:near]
            R1[0, pl.ds(row1 - pad1, near, stride=2), :] = value
            R1[0, pl.ds(row1 - pad1 + 1, near, stride=2), :] = value
            both = R1[0]
            A1[2 * i] = X1[2 * i] + both
            A1[2 * i + 1] = X1[2 * i + 1] + both
            return carry

        lax.fori_loop(0, b2x + 4, rise2, 0)
        L1.half(A1, 2, b1x + 4, True, store_to(B1))
        L1.half(B1, 3, b1x + 2, False, store_to(A1))

        def rise1(i, carry):
            value = A1[i, pl.ds(row1 - pad1, b1y + 2 * pad1), :]
            R0[i, pl.ds(0, b1y + 2 * pad1, stride=2), :] = value
            R0[i, pl.ds(1, b1y + 2 * pad1, stride=2), :] = value
            both = R0[i]
            B0[2 * i] = B0[2 * i] + both
            B0[2 * i + 1] = B0[2 * i + 1] + both
            return carry

        lax.fori_loop(pad1 - 1, pad1 + b1x + 1, rise1, 0)
        L0.half(B0, HALO - 1, bx + 2, True, store_to(A0))

        def accept(at, size, value):
            where = (pl.ds(at, size), pl.ds(HALO, by))
            U[where] = U[where] + value[:, HALO : HALO + by]

        L0.half(A0, HALO, bx, False, accept)

        @pl.when(k < NEWTON - 1)
        def _():
            for copy in exchange(U, bx, HALO, by, HALO, near_send, near_recv, k):
                copy.wait()

        return carry

    lax.fori_loop(0, NEWTON, newton, 0)
    out_ref[...] = U[pl.ds(HALO, bx), pl.ds(HALO, by)]


def per_device(gx, gy, density):
    bx, by, nz = density.shape
    e0 = (bx + 2 * HALO, by + 2 * HALO, nz)
    e1 = (bx // 2 + HALO, by // 2 + 2 * HALO, nz)
    e2 = (bx // 4 * gx + 4, by // 4 * gy, nz)
    e3 = (bx // 8 * gx + 4, by // 8 * gy, nz)
    field = lambda shape: pltpu.VMEM(shape, jnp.float32)
    sems = lambda *shape: pltpu.SemaphoreType.DMA(shape)
    scratch = [field(e0), field(e0), field((7,) + e0)] + [field(e0)] * 3
    scratch += [field((e0[0] // 2,) + e0[1:])]
    scratch += [field(e1), field((7,) + e1)] + [field(e1)] * 4 + [field(e1)]
    scratch += [field(e2), field((7,) + e2)] + [field(e2)] * 3 + [field(e2)]
    scratch += [field(e3), field((7,) + e3)] + [field(e3)] * 3
    scratch += [field((NEWTON + 1, gy, gx, 8, nz))]
    scratch += [sems(NEWTON, 8)] * 4
    scratch += [sems(NEWTON + 1, gx - 1)] * 2 + [sems(NEWTON + 1, gy - 1)] * 2
    return pl.pallas_call(
        functools.partial(kernel, gx, gy),
        out_shape=jax.ShapeDtypeStruct(density.shape, jnp.float32),
        in_specs=[pl.BlockSpec(memory_space=pltpu.VMEM)],
        out_specs=pl.BlockSpec(memory_space=pltpu.VMEM),
        scratch_shapes=scratch,
        compiler_params=pltpu.CompilerParams(
            collective_id=0, has_side_effects=True, vmem_limit_bytes=60 * 2**20
        ),
    )(density)


def solution(mesh):
    placed = P("gx", "gy", None)
    return jax.shard_map(
        functools.partial(per_device, mesh.shape["gx"], mesh.shape["gy"]),
        mesh=mesh, in_specs=(placed,), out_specs=placed, check_vma=False,
    )
```

time: 728 us -> 110 us (0.15)
  waiting for transfers between devices: 316 us -> 0 us
  starting transfers between devices: 136 us -> 0 us
  blocking collectives: 110 us -> 0 us
  Pallas kernels: 0 us -> 108 us
  local copies, waits for them, and re-layouts: 107 us -> 1.57 us
  other arithmetic: 54.1 us -> 0 us
    ppermute x192 -> x0, waiting for transfers between devices: 316 us -> none  [the longest x96 226 us: extended(): before = lax.ppermute(last, axis, up)]
    ppermute x192 -> x0, starting transfers between devices: 136 us -> none  [the longest x96 77 us: extended(): before = lax.ppermute(last, axis, up)]
    pallas_call x0 -> x1, Pallas kernels: none -> 108 us  [per_device(): pl.pallas_call(functools.partial(kernel, gx, gy), out_shape=jax.ShapeDtyp...]
    reshape x21 -> x0, local copies, waits for them, and re-layouts: 85.2 us -> none  [the longest x12 62.2 us: restrict(): blocks = field.reshape(size_x // 2, 2, size_y // 2, 2, size_z // 2, 2)]
    all_gather x6 -> x0, blocking collectives: 68.1 us -> none  [the longest x3 38.5 us: cycle(): packed = lax.all_gather(packed, 'gx', axis=1, tiled=True)]
    psum x1 -> x0, blocking collectives: 42.1 us -> none  [per_device(): mass_total = lax.psum(jnp.sum(density), ('gx', 'gy'))]
    reduce_sum x19 -> x0, other arithmetic: 27.3 us -> none  [the longest x18 25.7 us: restrict(): return jnp.sum(blocks, axis=(1, 3, 5)) * 0.125]
    broadcast_in_dim x9 -> x0, local copies, waits for them, and re-layouts: 12.7 us -> none  [prolong(): jnp.broadcast_to(field[:, None, :, None, :, None], (size_x, 2, size_y, 2,...]
  transfers between devices with their start and end apart: 192 -> 0, of which waited for: 162 -> 0; matrix products, arithmetic and copies ran while one was open for 14% -> 0% of each run, Pallas kernels for 0% -> 0%
where the time goes in v1:
time: 110 us
  Pallas kernels  108 us (98%)
  local copies, waits for them, and re-layouts  1.57 us (1%)
    pallas_call x1, Pallas kernels, per_device(): pl.pallas_call(functools.partial(kernel, gx, gy), out_shape=jax.ShapeDtyp...  108 us

profile of v1, /device:TPU:0, one launch (start us, length us, event | category | flops | bytes accessed | tf_op | source)
XLA Modules:
  0.0 109.6 jit_solution(14811258478958574447)
XLA Ops:
  0.0 108.0 %shard_map.17 = f32[16,16,128]{2,1,0:T(8,128)} custom-call(f32[16,16,128]{2,1,0:T(8,128)} %density_ref.1), custom_call_target="tpu_custom_call" | custom-call | tf_op jit(solution)/shard_map/pallas_call | solution.py:441
  108.0 1.6 %copy.3 = f32[16,16,128]{2,1,0:T(8,128)} copy(f32[16,16,128]{2,1,0:T(8,128)} %shard_map.17) | data formatting | bytes 262144

commit v2 on v1

--- a/solution.py
+++ b/solution.py
@@ -11,36 +11,71 @@
 NEWTON = 3
 COUPLING = 0.1
 FLOOR = 3.0
+BLOCKS = 4
 HALO = 8
 MESH = pl.DeviceIdType.MESH
 
 
-def parts_of(block, step):
+def parts_near(ref, at, size, row, rows, step, zero):
+    def take(dx, dy):
+        return ref[pl.ds(at + dx, size), pl.ds(zero + (row + dy), rows), :]
+
+    lanes = ref.shape[2]
+
+    def slope_z(value):
+        return pltpu.roll(value, lanes - step, 2) - pltpu.roll(value, step, 2)
+
+    center, x_next, x_prev = take(0, 0), take(1, 0), take(-1, 0)
+    y_next, y_prev = take(0, 1), take(0, -1)
+    twice = center + center
+    xx = x_next + x_prev - twice
+    yy = y_next + y_prev - twice
+    zz = pltpu.roll(center, lanes - step, 2) + pltpu.roll(center, step, 2) - twice
+    xy = take(1, 1) - take(1, -1) - take(-1, 1) + take(-1, -1)
+    xz = slope_z(x_next - x_prev)
+    yz = slope_z(y_next - y_prev)
+    return center, xx, yy, zz, xy, xz, yz
+
+
+def parts_whole(ref, at, size, step):
+    block = ref[pl.ds(at - 1, size + 2)]
     rows, lanes = block.shape[1], block.shape[2]
-    center = block[1:-1]
+    period = lanes // BLOCKS
+
+    def z_pair(value):
+        cell = lax.broadcasted_iota(jnp.int32, value.shape, 2) & (period - 1)
+        forth = jnp.where(
+            cell >= period - step,
+            pltpu.roll(value, period - step, 2),
+            pltpu.roll(value, lanes - step, 2),
+        )
+        back = jnp.where(
+            cell < step,
+            pltpu.roll(value, lanes - period + step, 2),
+            pltpu.roll(value, step, 2),
+        )
+        return forth, back
+
+    def slope_y(value):
+        return pltpu.roll(value, rows - 1, 1) - pltpu.roll(value, 1, 1)
+
+    center, x_next, x_prev = block[1:-1], block[2:], block[:-2]
     twice = center + center
-    z_next = pltpu.roll(block, lanes - step, 2)
-    z_prev = pltpu.roll(block, step, 2)
-    y_next = pltpu.roll(block, rows - 1, 1)
-    y_prev = pltpu.roll(block, 1, 1)
-    slope_z = z_next - z_prev
-    slope_y = y_next - y_prev
-    xx = block[2:] + block[:-2] - twice
-    yy = y_next[1:-1] + y_prev[1:-1] - twice
-    zz = z_next[1:-1] + z_prev[1:-1] - twice
-    xy = slope_y[2:] - slope_y[:-2]
-    xz = slope_z[2:] - slope_z[:-2]
-    inner = slope_z[1:-1]
-    yz = pltpu.roll(inner, rows - 1, 1) - pltpu.roll(inner, 1, 1)
-    return center, xx, yy, zz, xy, xz, yz
-
-
-def red_of(shape, first, level):
+    z_next, z_prev = z_pair(center)
+    xx = x_next + x_prev - twice
+    yy = pltpu.roll(center, rows - 1, 1) + pltpu.roll(center, 1, 1) - twice
+    zz = z_next + z_prev - twice
+    slope_x = x_next - x_prev
+    forth, back = z_pair(slope_x)
+    return center, xx, yy, zz, slope_y(slope_x), forth - back, slope_y(z_next - z_prev)
+
+
+def red_of(shape, first, shift):
     total = (
         lax.broadcasted_iota(jnp.int32, shape, 0)
         + first
         + lax.broadcasted_iota(jnp.int32, shape, 1)
-        + (lax.broadcasted_iota(jnp.int32, shape, 2) >> level)
+        + (lax.broadcasted_iota(jnp.int32, shape, 2) >> shift)
     )
     return (total & 1) == 0
 
@@ -57,16 +92,26 @@
 
 
 class Level:
-    def __init__(self, level, pad, weights, target, va, vb):
-        self.level, self.pad = level, pad
+    def __init__(self, level, pad, whole, zero, weights, target, va, vb):
+        self.level, self.pad, self.whole, self.zero = level, pad, whole, zero
         self.weights, self.target, self.va, self.vb = weights, target, va, vb
-        self.step = 1 << level
+        self.shift = level - 2 if whole else level
+        self.step = 1 << self.shift
         self.scale = 0.25**level
 
-    def setup(self, u_ref, first, count, source_ref=None):
+    def parts(self, ref, at, size, row, rows):
+        if self.whole:
+            return parts_whole(ref, at, size, self.step)
+        return parts_near(ref, at, size, row, rows, self.step, self.zero)
+
+    def at_rows(self, at, size, row, rows):
+        if self.whole:
+            return (pl.ds(at, size),)
+        return (pl.ds(at, size), pl.ds(self.zero + row, rows), slice(None))
+
+    def setup(self, u_ref, first, count, row, rows, source_ref=None):
         def body(at, size):
-            block = u_ref[pl.ds(at - 1, size + 2)]
-            _, xx, yy, zz, xy, xz, yz = parts_of(block, self.step)
+            _, xx, yy, zz, xy, xz, yz = self.parts(u_ref, at, size, row, rows)
             if self.level > 0:
                 xx, yy, zz = xx * self.scale, yy * self.scale, zz * self.scale
             quarter = 0.25 * self.scale
@@ -76,52 +121,52 @@
             kz = 1.0 + 2.0 * COUPLING * (xx + yy)
             diagonal = jnp.maximum(2.0 * (kx + ky + kz), FLOOR)
             relax = 1.0 / (self.scale * diagonal)
-            rows = pl.ds(at, size)
+            where = self.at_rows(at, size, row, rows)
             if source_ref is not None:
                 cubic = 2.0 * (xx * yy + xx * zz + yy * zz - xy * xy - xz * xz - yz * yz)
-                target = source_ref[rows] - (xx + yy + zz + COUPLING * cubic)
-                self.target[rows] = target
+                target = source_ref[where] - (xx + yy + zz + COUPLING * cubic)
+                self.target[where] = target
             else:
-                target = self.target[rows]
+                target = self.target[where]
             mixed = -4.0 * COUPLING * quarter
-            self.weights[0, rows] = kx * self.scale
-            self.weights[1, rows] = ky * self.scale
-            self.weights[2, rows] = kz * self.scale
-            self.weights[3, rows] = xy * mixed
-            self.weights[4, rows] = xz * mixed
-            self.weights[5, rows] = yz * mixed
-            self.weights[6, rows] = relax
-            red = red_of(target.shape, (first - self.pad) % 2, self.level)
-            self.va[rows] = jnp.where(red, -target * relax, 0.0)
+            self.weights[(0,) + where] = kx * self.scale
+            self.weights[(1,) + where] = ky * self.scale
+            self.weights[(2,) + where] = kz * self.scale
+            self.weights[(3,) + where] = xy * mixed
+            self.weights[(4,) + where] = xz * mixed
+            self.weights[(5,) + where] = yz * mixed
+            self.weights[(6,) + where] = relax
+            red = red_of(target.shape, (first - self.pad + row) % 2, self.shift)
+            self.va[where] = jnp.where(red, -target * relax, 0.0)
 
         planes(first, count, body)
 
-    def excess(self, v_ref, at, size):
-        block = v_ref[pl.ds(at - 1, size + 2)]
-        center, xx, yy, zz, xy, xz, yz = parts_of(block, self.step)
-        rows = pl.ds(at, size)
-        w = self.weights
-        total = w[0, rows] * xx + w[1, rows] * yy + w[2, rows] * zz
-        total += w[3, rows] * xy + w[4, rows] * xz + w[5, rows] * yz
-        return total - self.target[rows], center
-
-    def half(self, src, first, count, red, put):
+    def excess(self, v_ref, at, size, row, rows):
+        center, xx, yy, zz, xy, xz, yz = self.parts(v_ref, at, size, row, rows)
+        where = self.at_rows(at, size, row, rows)
+        w = lambda index: self.weights[(index,) + where]
+        total = w(0) * xx + w(1) * yy + w(2) * zz
+        total += w(3) * xy + w(4) * xz + w(5) * yz
+        return total - self.target[where], center
+
+    def half(self, src, first, count, row, rows, red, put):
         def body(at, size):
-            excess, center = self.excess(src, at, size)
-            change = excess * self.weights[6, pl.ds(at, size)]
-            mask = red_of(change.shape, (first - self.pad) % 2, self.level)
+            excess, center = self.excess(src, at, size, row, rows)
+            where = self.at_rows(at, size, row, rows)
+            change = excess * self.weights[(6,) + where]
+            mask = red_of(change.shape, (first - self.pad + row) % 2, self.shift)
             if red:
                 value = jnp.where(mask, center + change, center)
             else:
                 value = jnp.where(mask, center, center + change)
-            put(at, size, value)
+            put(where, value)
 
         planes(first, count, body)
 
 
 def store_to(ref):
-    def put(at, size, value):
-        ref[pl.ds(at, size)] = value
+    def put(where, value):
+        ref[where] = value
 
     return put
 
@@ -149,10 +194,10 @@
     lax.fori_loop(0, count, body, 0)
 
 
-def wrap_planes(ref, pad, count):
-    for i in range(pad):
-        ref[i] = ref[count + i]
-        ref[pad + count + i] = ref[pad + i]
+def wrap_planes(ref, count):
+    lanes = ref.shape[2]
+    ref[0] = pltpu.roll(ref[count], lanes // BLOCKS, 1)
+    ref[count + 1] = pltpu.roll(ref[1], lanes - lanes // BLOCKS, 1)
 
 
 def kernel(
@@ -170,7 +215,9 @@
     b1x, b1y = bx // 2, by // 2
     b2x, b2y = bx // 4, by // 4
     n2x, n2y = b2x * gx, b2y * gy
-    n3x, n3y = n2x // 2, n2y // 2
+    p2, p3, n3y = n2x // BLOCKS, n2x // (2 * BLOCKS), n2y // 2
+    ahead = gx // BLOCKS
+    zero = lax.div(me_y, gy)
     row1 = HALO
 
     def device(dx, dy):
@@ -261,10 +308,10 @@
 
     lax.fori_loop(0, bx + 2 * HALO, to_source, 0)
 
-    L0 = Level(0, HALO, W0, T0, A0, B0)
-    L1 = Level(1, pad1, W1, T1, A1, B1)
-    L2 = Level(2, 2, W2, T2, A2, B2)
-    L3 = Level(3, 2, W3, T3, A3, B3)
+    L0 = Level(0, HALO, False, zero, W0, T0, A0, B0)
+    L1 = Level(1, pad1, False, zero, W1, T1, A1, B1)
+    L2 = Level(2, 1, True, zero, W2, T2, A2, B2)
+    L3 = Level(3, 1, True, zero, W3, T3, A3, B3)
 
     lane_in = lax.broadcasted_iota(jnp.int32, (nz, nz), 0)
     lane_out = lax.broadcasted_iota(jnp.int32, (nz, nz), 1)
@@ -277,15 +324,15 @@
         )
 
     def newton(k, carry):
-        L0.setup(U, 2, bx + 12, S)
-        L0.half(A0, 3, bx + 10, False, store_to(B0))
+        L0.setup(U, 2, bx + 12, 2, by + 12, S)
+        L0.half(A0, 3, bx + 10, 3, by + 10, False, store_to(B0))
 
         def leftover0(at, size):
-            excess, _ = L0.excess(B0, at, size)
-            R0[pl.ds(at // 2, size // 2)] = pair_xz(-excess, 1)
+            excess, _ = L0.excess(B0, at, size, 4, by + 8)
+            R0[pl.ds(at // 2, size // 2), pl.ds(0, by + 8)] = pair_xz(-excess, 1)
 
         planes(4, bx + 8, leftover0)
-        pair_y(R0, 2, b1x + 4, by + 2 * HALO, T1, 2, row1 - pad1)
+        pair_y(R0, 2, b1x + 4, by + 8, T1, 2, row1 - 2)
 
         def shrink0(at, size):
             R0[pl.ds(at // 2, size // 2)] = pair_xz(U[pl.ds(at, size)], 1)
@@ -293,14 +340,14 @@
         planes(0, bx + 2 * HALO, shrink0)
         pair_y(R0, 0, b1x + 2 * pad1, by + 2 * HALO, U1, 0, row1 - pad1)
 
-        L1.setup(U1, 2, b1x + 4)
-        L1.half(A1, 3, b1x + 2, False, store_to(B1))
+        L1.setup(U1, 2, b1x + 4, row1 - 2, b1y + 4)
+        L1.half(A1, 3, b1x + 2, row1 - 1, b1y + 2, False, store_to(B1))
         X1[pl.ds(pad1, b1x), pl.ds(row1, b1y)] = B1[pl.ds(pad1, b1x), pl.ds(row1, b1y)]
         mid_copies = exchange(X1, b1x, pad1, b1y, row1, mid_send, mid_recv, k)
 
         def leftover1(at, size):
-            excess, _ = L1.excess(B1, at, size)
-            R1[pl.ds((at - pad1) // 2, size // 2)] = pair_xz(-excess, 2)
+            excess, _ = L1.excess(B1, at, size, row1, b1y)
+            R1[pl.ds((at - pad1) // 2, size // 2), pl.ds(row1, b1y)] = pair_xz(-excess, 2)
 
         planes(pad1, b1x, leftover1)
 
@@ -322,76 +369,82 @@
         G[k, me_y, me_x] = message
         gather(k)
 
-        packed = G[k].reshape(gy * gx * 2 * b2y, nz)
+        group = lax.broadcasted_iota(jnp.int32, (gy, ahead, 2 * b2y, nz), 3) // width
         rights, fields = [], []
         for i in range(b2x):
-            spread = (lane_in == (lane_out >> 2) + i * width).astype(jnp.float32)
-            cells = dot(packed, spread).reshape(gy, gx, 2 * b2y, nz)
+            cells = None
+            for block in range(BLOCKS):
+                part = G[k, :, block * ahead : (block + 1) * ahead]
+                turn = (block - i) * width % nz
+                if turn:
+                    part = pltpu.roll(part, turn, 3)
+                cells = part if cells is None else jnp.where(group == block, part, cells)
             rights.append(jnp.concatenate([cells[j, :, :b2y] for j in range(gy)], axis=1))
             fields.append(jnp.concatenate([cells[j, :, b2y:] for j in range(gy)], axis=1))
-        T2[pl.ds(2, n2x)] = jnp.stack(rights, axis=1).reshape(n2x, n2y, nz)
-        U2[pl.ds(2, n2x)] = jnp.stack(fields, axis=1).reshape(n2x, n2y, nz)
-        wrap_planes(U2, 2, n2x)
-
-        L2.setup(U2, 2, n2x)
-        wrap_planes(A2, 2, n2x)
-        L2.half(A2, 2, n2x, False, store_to(B2))
-        wrap_planes(B2, 2, n2x)
+        T2[pl.ds(1, p2)] = jnp.stack(rights, axis=1).reshape(p2, n2y, nz)
+        U2[pl.ds(1, p2)] = jnp.stack(fields, axis=1).reshape(p2, n2y, nz)
+        wrap_planes(U2, p2)
+
+        L2.setup(U2, 1, p2, 0, n2y)
+        wrap_planes(A2, p2)
+        L2.half(A2, 1, p2, 0, n2y, False, store_to(B2))
+        wrap_planes(B2, p2)
 
         def leftover2(at, size):
-            excess, _ = L2.excess(B2, at, size)
-            R2[pl.ds((at - 2) // 2, size // 2)] = pair_xz(-excess, 4)
-
-        planes(2, n2x, leftover2)
-        pair_y(R2, 0, n3x, n2y, T3, 2, 0)
+            excess, _ = L2.excess(B2, at, size, 0, n2y)
+            R2[pl.ds((at - 1) // 2, size // 2)] = pair_xz(-excess, 1)
+
+        planes(1, p2, leftover2)
+        pair_y(R2, 0, p3, n2y, T3, 1, 0)
 
         def shrink2(at, size):
-            R2[pl.ds((at - 2) // 2, size // 2)] = pair_xz(U2[pl.ds(at, size)], 4)
-
-        planes(2, n2x, shrink2)
-        pair_y(R2, 0, n3x, n2y, U3, 2, 0)
-        wrap_planes(U3, 2, n3x)
-        L3.setup(U3, 2, n3x)
-        wrap_planes(A3, 2, n3x)
-        L3.half(A3, 2, n3x, False, store_to(B3))
-        wrap_planes(B3, 2, n3x)
-        L3.half(B3, 2, n3x, True, store_to(A3))
-        wrap_planes(A3, 2, n3x)
-        L3.half(A3, 2, n3x, False, store_to(B3))
-
-        def rise3(i, carry):
-            value = B3[2 + i]
+            R2[pl.ds((at - 1) // 2, size // 2)] = pair_xz(U2[pl.ds(at, size)], 1)
+
+        planes(1, p2, shrink2)
+        pair_y(R2, 0, p3, n2y, U3, 1, 0)
+        wrap_planes(U3, p3)
+        L3.setup(U3, 1, p3, 0, n3y)
+        wrap_planes(A3, p3)
+        L3.half(A3, 1, p3, 0, n3y, False, store_to(B3))
+        wrap_planes(B3, p3)
+        L3.half(B3, 1, p3, 0, n3y, True, store_to(A3))
+        wrap_planes(A3, p3)
+        L3.half(A3, 1, p3, 0, n3y, False, store_to(B3))
+
+        for i in range(p3):
+            value = B3[1 + i]
             R2[i, pl.ds(0, n3y, stride=2), :] = value
             R2[i, pl.ds(1, n3y, stride=2), :] = value
             both = R2[i]
+            B2[1 + 2 * i] = B2[1 + 2 * i] + both
             B2[2 + 2 * i] = B2[2 + 2 * i] + both
-            B2[3 + 2 * i] = B2[3 + 2 * i] + both
-            return carry
-
-        lax.fori_loop(0, n3x, rise3, 0)
-        wrap_planes(B2, 2, n2x)
-        L2.half(B2, 2, n2x, True, store_to(A2))
-        wrap_planes(A2, 2, n2x)
-        L2.half(A2, 2, n2x, False, store_to(B2))
-        wrap_planes(B2, 2, n2x)
+        wrap_planes(B2, p2)
+        L2.half(B2, 1, p2, 0, n2y, True, store_to(A2))
+        wrap_planes(A2, p2)
+        L2.half(A2, 1, p2, 0, n2y, False, store_to(B2))
 
         for copy in mid_copies:
             copy.wait()
         near = b2y + 4
         shift = lax.rem(n2y - me_y * b2y + 2, n2y)
-
-        def rise2(i, carry):
-            value = pltpu.roll(B2[me_x * b2x + i], shift, 0)[:near]
+        taken = []
+        for i in range(b2x + 4):
+            plane = lax.rem(me_x * b2x + (n2x - 2 + i), n2x)
+            value = B2[1 + lax.rem(plane, p2)]
+            value = pltpu.roll(value, shift, 0)[:near]
+            taken.append(pltpu.roll(value, lax.rem(nz - lax.div(plane, p2) * width, nz), 1))
+        spread = (lane_in == (lane_out >> 2)).astype(jnp.float32)
+        taken = dot(jnp.concatenate(taken, axis=0), spread)
+        for i in range(b2x + 4):
+            value = taken[i * near : (i + 1) * near]
             R1[0, pl.ds(row1 - pad1, near, stride=2), :] = value
             R1[0, pl.ds(row1 - pad1 + 1, near, stride=2), :] = value
             both = R1[0]
             A1[2 * i] = X1[2 * i] + both
             A1[2 * i + 1] = X1[2 * i + 1] + both
-            return carry
-
-        lax.fori_loop(0, b2x + 4, rise2, 0)
-        L1.half(A1, 2, b1x + 4, True, store_to(B1))
-        L1.half(B1, 3, b1x + 2, False, store_to(A1))
+
+        L1.half(A1, 2, b1x + 4, row1 - 2, b1y + 4, True, store_to(B1))
+        L1.half(B1, 3, b1x + 2, row1 - 1, b1y + 2, False, store_to(A1))
 
         def rise1(i, carry):
             value = A1[i, pl.ds(row1 - pad1, b1y + 2 * pad1), :]
@@ -403,13 +456,12 @@
             return carry
 
         lax.fori_loop(pad1 - 1, pad1 + b1x + 1, rise1, 0)
-        L0.half(B0, HALO - 1, bx + 2, True, store_to(A0))
-
-        def accept(at, size, value):
-            where = (pl.ds(at, size), pl.ds(HALO, by))
-            U[where] = U[where] + value[:, HALO : HALO + by]
-
-        L0.half(A0, HALO, bx, False, accept)
+        L0.half(B0, HALO - 1, bx + 2, HALO - 1, by + 2, True, store_to(A0))
+
+        def accept(where, value):
+            U[where] = U[where] + value
+
+        L0.half(A0, HALO, bx, HALO, by, False, accept)
 
         @pl.when(k < NEWTON - 1)
         def _():
@@ -426,8 +478,8 @@
     bx, by, nz = density.shape
     e0 = (bx + 2 * HALO, by + 2 * HALO, nz)
     e1 = (bx // 2 + HALO, by // 2 + 2 * HALO, nz)
-    e2 = (bx // 4 * gx + 4, by // 4 * gy, nz)
-    e3 = (bx // 8 * gx + 4, by // 8 * gy, nz)
+    e2 = (bx // 4 * gx // BLOCKS + 2, by // 4 * gy, nz)
+    e3 = (bx // 8 * gx // BLOCKS + 2, by // 8 * gy, nz)
     field = lambda shape: pltpu.VMEM(shape, jnp.float32)
     sems = lambda *shape: pltpu.SemaphoreType.DMA(shape)
     scratch = [field(e0), field(e0), field((7,) + e0)] + [field(e0)] * 3

time: 110 us -> 94.2 us (0.86)
  Pallas kernels: 108 us -> 92.5 us
    pallas_call x1, Pallas kernels: 108 us -> 92.5 us  [per_device(): pl.pallas_call(functools.partial(kernel, gx, gy), out_shape=jax.ShapeDtyp...]
where the time goes in v2:
time: 94.2 us; the launch traced here: 94.1 us
  Pallas kernels  92.5 us (98%)
  local copies, waits for them, and re-layouts  1.57 us (2%)
    pallas_call x1, Pallas kernels, per_device(): pl.pallas_call(functools.partial(kernel, gx, gy), out_shape=jax.ShapeDtyp...  92.5 us

profile of v2, /device:TPU:0, one launch (start us, length us, event | category | flops | bytes accessed | tf_op | source)
XLA Modules:
  0.0 94.1 jit_solution(13784657599738442822)
XLA Ops:
  0.0 92.5 %shard_map.17 = f32[16,16,128]{2,1,0:T(8,128)} custom-call(f32[16,16,128]{2,1,0:T(8,128)} %density_ref.1), custom_call_target="tpu_custom_call" | custom-call | tf_op jit(solution)/shard_map/pallas_call | solution.py:493
  92.5 1.6 %copy.3 = f32[16,16,128]{2,1,0:T(8,128)} copy(f32[16,16,128]{2,1,0:T(8,128)} %shard_map.17) | data formatting | bytes 262144

commit v3 on v2

--- a/solution.py
+++ b/solution.py
@@ -88,7 +88,7 @@
         body(first + i * size, size)
         return carry
 
-    lax.fori_loop(0, count // size, turn, 0)
+    lax.fori_loop(0, count // size, turn, 0, unroll=True)
 
 
 class Level:
@@ -191,7 +191,7 @@
         out[out_first + i, pl.ds(out_row, half), :] = (low + high) * 0.125
         return carry
 
-    lax.fori_loop(0, count, body, 0)
+    lax.fori_loop(0, count, body, 0, unroll=True)
 
 
 def wrap_planes(ref, count):
@@ -306,7 +306,7 @@
         S[i] = S[i] / mean - 1.0
         return carry
 
-    lax.fori_loop(0, bx + 2 * HALO, to_source, 0)
+    lax.fori_loop(0, bx + 2 * HALO, to_source, 0, unroll=4)
 
     L0 = Level(0, HALO, False, zero, W0, T0, A0, B0)
     L1 = Level(1, pad1, False, zero, W1, T1, A1, B1)
@@ -455,7 +455,7 @@
             B0[2 * i + 1] = B0[2 * i + 1] + both
             return carry
 
-        lax.fori_loop(pad1 - 1, pad1 + b1x + 1, rise1, 0)
+        lax.fori_loop(pad1 - 1, pad1 + b1x + 1, rise1, 0, unroll=True)
         L0.half(B0, HALO - 1, bx + 2, HALO - 1, by + 2, True, store_to(A0))
 
         def accept(where, value):

time: 94.2 us -> 77.3 us (0.82)
  Pallas kernels: 92.5 us -> 75.6 us
    pallas_call x1, Pallas kernels: 92.5 us -> 75.6 us  [per_device(): pl.pallas_call(functools.partial(kernel, gx, gy), out_shape=jax.ShapeDtyp...]
where the time goes in v3:
time: 77.3 us; the launch traced here: 77.2 us
  Pallas kernels  75.6 us (98%)
  local copies, waits for them, and re-layouts  1.57 us (2%)
    pallas_call x1, Pallas kernels, per_device(): pl.pallas_call(functools.partial(kernel, gx, gy), out_shape=jax.ShapeDtyp...  75.6 us
    unnamed x1, local copies, waits for them, and re-layouts  1.57 us

profile of v3, /device:TPU:0, one launch (start us, length us, event | category | flops | bytes accessed | tf_op | source)
XLA Modules:
  0.0 77.2 jit_solution(13815083519727403887)
XLA Ops:
  0.0 75.6 %shard_map.17 = f32[16,16,128]{2,1,0:T(8,128)} custom-call(f32[16,16,128]{2,1,0:T(8,128)} %density_ref.1), custom_call_target="tpu_custom_call" | custom-call | tf_op jit(solution)/shard_map/pallas_call | solution.py:493
  75.6 1.6 %copy.3 = f32[16,16,128]{2,1,0:T(8,128)} copy(f32[16,16,128]{2,1,0:T(8,128)} %shard_map.17) | data formatting | bytes 262144
